TPU v7x, 32 devices: a whole 2x2x4 slice. The times are simulated.
32 devices in a mesh: gx: 4 (over x, core), gy: 8 (over z, y).
Axes of the slice: x: 2, y: 2, z: 4, core: 2. Of those that a mesh axis runs over, the one named last changes fastest.
Arguments:
- velocity: float32 [3, 1024, 512], P(None, ('gx', 'gy')), may hold values from -6 to 6
- depart: float32 [3, 524288], P(None, ('gx', 'gy')), may hold values from -1 to 1
- owner_rank: int32 [524288, 1], P(('gx', 'gy')), may hold values from 0 to 31; in each aligned block of 16384 rows (0 to 16383, 16384 to 32767, ...) at most 1024 rows name the same one
- owner_element_index: int32 [524288], P(('gx', 'gy')), may hold values from 0 to 31
- neighbours: int32 [6, 1024], P(None, ('gx', 'gy')), may hold values from -1 to 1023, as said below
Outputs:
- advected: float32 [3, 1024, 512], P(None, ('gx', 'gy'))
Inputs may be any that keep to these rules, and one draw needn't show every extreme that they name: `owner_rank`: within the rows of one device no owner device is named by more than 1024 rows, and in some device's rows one owner is named exactly 1024 times. `neighbours`: -1 marks a boundary face; any other entry is an element of the same block of 32 consecutive elements as the entry's own element, or of the block just before or just after it.
All inputs are finite; a program needn't handle non-finite values.
Results may differ from a plain program's by a relative error of at most 0.0003.
Values sent between devices are 32-bit elements; how exact they have to be, the bound alone decides.
A program may use at most 64 MiB of HBM per device.

v0:
```python
import functools
import math

import jax
import jax.numpy as jnp
import numpy as np
from jax import lax
from jax.experimental import pallas as pl
from jax.experimental.pallas import tpu as pltpu
from jax.sharding import PartitionSpec as P

GLL_POINTS = np.array(
    [
        -1.0,
        -0.8717401485096066,
        -0.5917001814331423,
        -0.2092992179024789,
        0.2092992179024789,
        0.5917001814331423,
        0.8717401485096066,
        1.0,
    ]
)
F32, BF16 = jnp.float32, jnp.bfloat16
MESH = pl.DeviceIdType.MESH


def lagrange_constants():
    table = np.zeros((8, 128))
    for i in range(8):
        table[i, 0] = 1.0 / np.prod([GLL_POINTS[i] - GLL_POINTS[m] for m in range(8) if m != i])
        for r in range(1, 8):
            table[i, r] = GLL_POINTS[(i + r) % 8]
    return table.astype(np.float32)


def face_selector():
    cube = np.arange(512).reshape(8, 8, 8)
    faces = [cube[0], cube[7], cube[:, 0], cube[:, 7], cube[:, :, 0], cube[:, :, 7]]
    nodes = np.concatenate([face.reshape(-1) for face in faces])
    return (np.arange(512)[:, None] == nodes[None, :]).astype(np.float32)


def split2(x):
    hi = x.astype(BF16).astype(F32)
    return hi, x - hi


def dot(a, b):
    return lax.dot_general(a, b, (((1,), (0,)), ((), ())), preferred_element_type=F32)


def dot_nt(a, b):
    return lax.dot_general(a, b, (((1,), (1,)), ((), ())), preferred_element_type=F32)


def one_hot_rows(slot, capacity):
    width = slot.shape[1]
    rows = lax.broadcasted_iota(jnp.int32, (capacity, 128), 0).astype(jnp.int16)
    rows = jnp.concatenate([rows] * (width // 128), axis=1)
    slots = jnp.broadcast_to(slot, (16, width)).astype(jnp.int16)
    slots = jnp.concatenate([slots] * (capacity // 16), axis=0)
    return jnp.where(rows == slots, jnp.array(1, BF16), jnp.array(0, BF16))


def place_step(peers, capacity, sub, owner_ref, coords_ref, elem_ref, upper_ref, slot_ref, acc, carry):
    @pl.when(pl.program_id(0) == 0)
    def _():
        acc[...] = jnp.zeros_like(acc)
        carry[...] = jnp.zeros_like(carry)

    block = owner_ref.shape[1]
    upper = upper_ref[...]
    peer_rows = lax.broadcasted_iota(jnp.int32, (peers, sub), 0)
    slots = []
    running = carry[:, 0:1]
    for part in range(block // sub):
        owner = owner_ref[:, part * sub : (part + 1) * sub]
        match = peer_rows == owner
        hot = match.astype(F32)
        earlier = dot(hot.astype(BF16), upper) + running
        slots.append(jnp.sum(jnp.where(match, earlier, 0.0), axis=0, keepdims=True))
        running = running + jnp.sum(hot, axis=1, keepdims=True)
    carry[...] = jnp.broadcast_to(running, carry.shape)
    slot = jnp.concatenate(slots, axis=1).astype(jnp.int32)
    slot_ref[...] = slot
    owner = jnp.broadcast_to(owner_ref[...], (8, block))
    hi, lo = split2(coords_ref[...])
    values = jnp.concatenate([hi, elem_ref[...].astype(F32), lo, jnp.zeros((1, block), F32)], axis=0)
    spread = jnp.concatenate([jnp.where(owner == p, values, 0.0) for p in range(peers)], axis=0).astype(BF16)
    rows = lax.broadcasted_iota(jnp.int32, (capacity, block), 0)
    acc[...] += dot_nt((rows == slot).astype(F32).astype(BF16), spread)


def interp_chunks(elems, chunk, load, store, slots, stacked, const_ref):
    for at in range(0, slots, chunk):
        x = load(slice(at, at + chunk))
        weights = []
        for d in range(3):
            coord = jnp.broadcast_to(x[d : d + 1], (8, chunk))
            w = const_ref[:, 0:1] * (coord - const_ref[:, 1:2])
            for r in range(2, 8):
                w = w * (coord - const_ref[:, r : r + 1])
            weights.append(w)
        elem = jnp.broadcast_to(x[3:4], (8, chunk))
        hi, lo = split2(weights[2])
        picks = [elem == float(e) for e in range(elems)]
        a_hi = jnp.concatenate([jnp.where(pick, hi, 0.0) for pick in picks], axis=0).astype(BF16)
        a_lo = jnp.concatenate([jnp.where(pick, lo, 0.0) for pick in picks], axis=0).astype(BF16)
        summed = dot(stacked[...], jnp.concatenate([a_hi, a_lo, a_hi], axis=0))
        results = []
        for c in range(3):
            total = None
            for i in range(8):
                term = summed[64 * c + 8 * i : 64 * c + 8 * i + 8] * weights[0][i : i + 1]
                total = term if total is None else total + term
            results.append(jnp.sum(total * weights[1], axis=0, keepdims=True))
        store(slice(at, at + chunk), jnp.concatenate(results, axis=0))


def exchange_kernel(
    outer, inner, elems, chunk, sub, owner_ref, coords_ref, elem_ref, upper_ref, table_ref, const_ref,
    out_ref, slot_ref, acc, carry, send_ref, stacked, arrived, replies, landed, go_out, go_in, back_out, back_in,
):
    peers = outer * inner
    slots = out_ref.shape[2]
    my_x, my_y = lax.axis_index("gx"), lax.axis_index("gy")
    me = my_x * inner + my_y

    def after(s):
        x, y = lax.rem(my_x + lax.rem(s, outer), outer), lax.rem(my_y + s // outer, inner)
        return x, y, x * inner + y

    def before(s):
        x = lax.rem(my_x + outer - lax.rem(s, outer), outer)
        y = lax.rem(my_y + inner - s // outer, inner)
        return x, y, x * inner + y

    barrier = pltpu.get_barrier_semaphore()

    @pl.when(pl.program_id(0) == 0)
    def _():
        @pl.loop(1, peers)
        def _(s):
            x, y, _ = after(s)
            pl.semaphore_signal(barrier, inc=1, device_id=(x, y), device_id_type=MESH)

        hi, lo = split2(table_ref[...])
        stacked[...] = jnp.concatenate([hi, hi, lo], axis=1).astype(BF16)

    place_step(peers, slots, sub, owner_ref, coords_ref, elem_ref, upper_ref, slot_ref, acc, carry)

    def outgoing(s):
        x, y, target = after(s)
        return pltpu.make_async_remote_copy(
            src_ref=send_ref.at[target], dst_ref=arrived.at[me],
            send_sem=go_out.at[target], recv_sem=go_in.at[me],
            device_id=(x, y), device_id_type=MESH,
        )

    def incoming(s):
        x, y, source = before(s)
        return pltpu.make_async_remote_copy(
            src_ref=send_ref.at[source], dst_ref=arrived.at[source],
            send_sem=go_out.at[source], recv_sem=go_in.at[source],
            device_id=(x, y), device_id_type=MESH,
        )

    def reply(s):
        x, y, source = before(s)
        return pltpu.make_async_remote_copy(
            src_ref=replies.at[source], dst_ref=landed.at[me],
            send_sem=back_out.at[source], recv_sem=back_in.at[me],
            device_id=(x, y), device_id_type=MESH,
        )

    def answer(s):
        x, y, target = after(s)
        return pltpu.make_async_remote_copy(
            src_ref=replies.at[target], dst_ref=landed.at[target],
            send_sem=back_out.at[target], recv_sem=back_in.at[target],
            device_id=(x, y), device_id_type=MESH,
        )

    @pl.when(pl.program_id(0) == pl.num_programs(0) - 1)
    def _():
        turned = acc[...].T
        for p in range(peers):
            both = turned[8 * p : 8 * p + 8]
            send_ref[p] = jnp.concatenate([both[0:3] + both[4:7], both[3:4]], axis=0)
        pl.semaphore_wait(barrier, peers - 1)

        @pl.loop(1, peers)
        def _(s):
            outgoing(s).start()

        def own_store(where, value):
            out_ref[me, :, where] = value

        interp_chunks(elems, chunk, lambda where: send_ref[me, :, where], own_store, slots, stacked, const_ref)

        @pl.loop(1, peers)
        def _(s):
            _, _, source = before(s)
            incoming(s).wait_recv()

            def store(where, value):
                replies[source, :, where] = value

            interp_chunks(elems, chunk, lambda where: arrived[source, :, where], store, slots, stacked, const_ref)

            @pl.when(s > 1)
            def _():
                reply(s - 1).start()

        @pl.loop(1, peers)
        def _(s):
            outgoing(s).wait_send()

        reply(peers - 1).start()

        @pl.loop(1, peers)
        def _(s):
            _, _, target = after(s)
            answer(s).wait_recv()
            out_ref[target] = landed[target]

        @pl.loop(1, peers)
        def _(s):
            reply(s).wait_send()


def exchange(owner, coords, elem, table, outer, inner, capacity):
    peers = outer * inner
    points = owner.shape[1]
    elems = table.shape[1] // 8
    chunk = math.gcd(capacity, 256)
    block, sub = math.gcd(points, 4096), math.gcd(points, 256)
    upper = np.triu(np.ones((sub, sub), np.float32), 1)
    whole = lambda i: (0, 0)
    return pl.pallas_call(
        functools.partial(exchange_kernel, outer, inner, elems, chunk, sub),
        grid=(points // block,),
        in_specs=[
            pl.BlockSpec((1, block), lambda i: (0, i)),
            pl.BlockSpec((3, block), lambda i: (0, i)),
            pl.BlockSpec((1, block), lambda i: (0, i)),
            pl.BlockSpec((sub, sub), whole),
            pl.BlockSpec(table.shape, whole),
            pl.BlockSpec((8, 128), whole),
        ],
        out_specs=[
            pl.BlockSpec((peers, 3, capacity), lambda i: (0, 0, 0)),
            pl.BlockSpec((1, block), lambda i: (0, i)),
        ],
        out_shape=[
            jax.ShapeDtypeStruct((peers, 3, capacity), F32),
            jax.ShapeDtypeStruct((1, points), jnp.int32),
        ],
        scratch_shapes=[
            pltpu.VMEM((capacity, 8 * peers), F32),
            pltpu.VMEM((peers, 128), F32),
            pltpu.VMEM((peers, 4, capacity), F32),
            pltpu.VMEM((192, 3 * table.shape[1]), BF16),
            pltpu.VMEM((peers, 4, capacity), F32),
            pltpu.VMEM((peers, 3, capacity), F32),
            pltpu.VMEM((peers, 3, capacity), F32),
        ] + [pltpu.SemaphoreType.DMA((peers,))] * 4,
        compiler_params=pltpu.CompilerParams(
            dimension_semantics=("arbitrary",), collective_id=0, has_side_effects=True
        ),
        name="exchange",
    )(owner, coords, elem, jnp.asarray(upper, BF16), table, jnp.asarray(lagrange_constants()))


def finish_kernel(
    outer, inner, per_step, answers_ref, owner_ref, slot_ref, select_ref, index_ref, out_ref,
    halves, faces, below, above, send_sem, recv_sem,
):
    step = pl.program_id(0)
    peers = outer * inner
    capacity = answers_ref.shape[2]
    elems = out_ref.shape[1]
    me = lax.axis_index("gx") * inner + lax.axis_index("gy")
    up, down = lax.rem(me + 1, peers), lax.rem(me + peers - 1, peers)
    barrier = pltpu.get_barrier_semaphore()

    def place_of(device):
        return (device // inner, lax.rem(device, inner))

    @pl.when(step == 0)
    def _():
        for device in (up, down):
            pl.semaphore_signal(barrier, inc=1, device_id=place_of(device), device_id_type=MESH)
        for c in range(3):
            hi, lo = split2(answers_ref[:, c, :])
            halves[peers * c : peers * (c + 1)] = hi.astype(BF16)
            halves[peers * (c + 3) : peers * (c + 4)] = lo.astype(BF16)

    for at in range(per_step):
        nodes = slice(512 * at, 512 * at + 512)
        picked = dot(halves[...], one_hot_rows(slot_ref[:, nodes], capacity))
        match = lax.broadcasted_iota(jnp.int32, (peers, 512), 0) == owner_ref[:, nodes]
        for c in range(3):
            both = picked[peers * c : peers * (c + 1)] + picked[peers * (c + 3) : peers * (c + 4)]
            value = jnp.sum(jnp.where(match, both, 0.0), axis=0, keepdims=True)
            out_ref[c, pl.ds(step * per_step + at, 1), :] = value

    @pl.when(step == pl.num_programs(0) - 1)
    def _():
        sel = select_ref[...]
        copies = [
            [
                pltpu.make_async_remote_copy(
                    src_ref=faces.at[c], dst_ref=land.at[c],
                    send_sem=send_sem.at[2 * c + k], recv_sem=recv_sem.at[2 * c + k],
                    device_id=place_of(device), device_id_type=MESH,
                )
                for k, (device, land) in enumerate(((up, below), (down, above)))
            ]
            for c in range(3)
        ]
        pl.semaphore_wait(barrier, 2)
        for c in range(3):
            hi, lo = split2(out_ref[c])
            mid, low = split2(lo)
            faces[c] = dot(hi.astype(BF16), sel) + dot(mid.astype(BF16), sel) + dot(low.astype(BF16), sel)
            if c > 0:
                for copy in copies[c - 1]:
                    copy.start()
        index = index_ref[...]
        columns = lax.broadcasted_iota(jnp.int32, (6 * elems, 3 * elems), 1)
        picker = (columns == index).astype(F32).astype(BF16)
        present = (index >= 0).astype(F32)
        for copy in copies[2]:
            copy.start()
        for c in range(3):
            for copy in copies[c]:
                copy.wait()
            own = faces[c]
            extended = jnp.concatenate([below[c], own, above[c]], axis=0)
            hi, lo = split2(extended)
            across = dot(picker, hi.astype(BF16)) + dot(picker, lo.astype(BF16))
            changes = []
            for f in range(6):
                g = f ^ 1
                rows = slice(f * elems, (f + 1) * elems)
                other = across[rows, 64 * g : 64 * g + 64]
                changes.append(0.5 * (other - present[rows] * own[:, 64 * f : 64 * f + 64]))
            hi, lo = split2(jnp.concatenate(changes, axis=1))
            out_ref[c] += dot_nt(hi.astype(BF16), sel) + dot_nt(lo.astype(BF16), sel)


def finish(answers, owner, slot, index, elems, outer, inner):
    peers, _, capacity = answers.shape
    points = owner.shape[1]
    per_step = math.gcd(elems, 8)
    block = per_step * 512
    return pl.pallas_call(
        functools.partial(finish_kernel, outer, inner, per_step),
        grid=(points // block,),
        in_specs=[
            pl.BlockSpec(answers.shape, lambda i: (0, 0, 0)),
            pl.BlockSpec((1, block), lambda i: (0, i)),
            pl.BlockSpec((1, block), lambda i: (0, i)),
            pl.BlockSpec((512, 384), lambda i: (0, 0)),
            pl.BlockSpec(index.shape, lambda i: (0, 0)),
        ],
        out_specs=pl.BlockSpec((3, elems, 512), lambda i: (0, 0, 0)),
        out_shape=jax.ShapeDtypeStruct((3, elems, 512), F32),
        scratch_shapes=[pltpu.VMEM((6 * peers, capacity), BF16)]
        + [pltpu.VMEM((3, elems, 384), F32)] * 3
        + [pltpu.SemaphoreType.DMA((6,))] * 2,
        compiler_params=pltpu.CompilerParams(
            dimension_semantics=("arbitrary",), collective_id=1, has_side_effects=True
        ),
        name="finish",
    )(answers, owner, slot, jnp.asarray(face_selector(), BF16), index)


def local(velocity, depart, owner_rank, owner_element_index, neighbours):
    outer, inner = lax.axis_size("gx"), lax.axis_size("gy")
    peers = outer * inner
    elems = velocity.shape[1]
    points = depart.shape[1]
    capacity = 2 * points // peers
    owner = owner_rank.reshape(1, points)
    table = velocity.reshape(3, elems, 64, 8).transpose(0, 2, 1, 3).reshape(192, elems * 8)
    elem = owner_element_index.reshape(1, points)
    answers, slot = exchange(owner, depart, elem, table, outer, inner, capacity)
    device_id = lax.axis_index("gx") * inner + lax.axis_index("gy")
    index = jnp.where(neighbours >= 0, neighbours - (device_id - 1) * elems, -1)
    return finish(answers, owner, slot, index.reshape(6 * elems, 1), elems, outer, inner)


def solution(mesh):
    placed = (
        P(None, ("gx", "gy"), None),
        P(None, ("gx", "gy")),
        P(("gx", "gy"), None),
        P(("gx", "gy")),
        P(None, ("gx", "gy")),
    )
    return jax.shard_map(
        local, mesh=mesh, in_specs=placed, out_specs=P(None, ("gx", "gy"), None), check_vma=False
    )
```

profile of v0, /device:TPU:0, one launch (start us, length us, event | category | flops | bytes accessed | tf_op | source)
XLA Modules:
  0.0 74.0 jit_solution(5818291543025595679)
XLA Ops:
  0.0 1.2 %copy.10 = f32[3,32,512]{1,2,0:T(8,128)S(1)} copy(f32[3,32,512]{2,1,0:T(8,128)} %param.8) | data formatting | bytes 393216 | tf_op args[0]
  1.2 0.7 copy.11
  1.9 0.3 reshape.18
  2.2 0.8 %copy.12.table_ref = f32[192,256]{1,0:T(8,128)} copy(f32[192,256]{0,1:T(8,128)S(1)} %reshape.18) | data formatting | bytes 393216 | tf_op jit(solution)/shard_map/reshape | solution.py:388
  3.0 49.9 %exchange.1 = (f32[32,3,1024]{2,1,0:T(4,128)}, s32[1,16384]{1,0:T(1,128)}) custom-call(s32[1,16384]{1,0:T(1,128)} %bitcast.8, f32[3,16384]{1,0:T(4,128)} %coords_ref.1, s32[1,16384]{1,0:T(1,128)} %bitcast.10, bf16[256,256]{1,0:T(8,128)(2,1)} %constant.24.clone.upper_ref, f32[192,256]{1,0:T(8,128)} %copy.12.table_ref, f32[8,128]{1,0:T(8,128)} %constant.25.clone.const_ref), custom_call_target="tpu_custom_call" | custom-call | tf_op jit(solution)/shard_map/exchange/pallas_call | solution.py:241
  52.9 0.0 copy-start
  52.9 0.7 copy-done
  53.6 0.8 %reshape.20.index_ref = s32[192,1]{1,0:T(8,128)} reshape(s32[6,32]{1,0:T(8,128)S(1)} %subtract_select_fusion) | data formatting | bytes 1536 | tf_op jit(solution)/shard_map/reshape | solution.py:393
  54.4 18.0 %finish.1 = f32[3,32,512]{2,1,0:T(8,128)} custom-call(f32[32,3,1024]{2,1,0:T(4,128)} %get-tuple-element.7.answers_ref, s32[1,16384]{1,0:T(1,128)} %bitcast.9, s32[1,16384]{1,0:T(1,128)} %get-tuple-element.8.slot_ref, bf16[512,384]{1,0:T(8,128)(2,1)} %constant.26.clone.select_ref, s32[192,1]{1,0:T(8,128)} %reshape.20.index_ref), custom_call_target="tpu_custom_call" | custom-call | tf_op jit(solution)/shard_map/finish/pallas_call | solution.py:359
  72.4 1.6 %copy.15 = f32[3,32,512]{2,1,0:T(8,128)} copy(f32[3,32,512]{2,1,0:T(8,128)} %finish.1) | data formatting | bytes 393216
  (1 shorter events, 0.0 us)
Async XLA Ops:
  52.9 0.7 copy-start
where the time goes:
time: 74.2 us; the launch traced here: 74 us
  Pallas kernels  67.9 us (92%)
  local copies, waits for them, and re-layouts  6.01 us (8%)
    pallas_call x1, Pallas kernels, exchange(): pl.pallas_call(functools.partial(exchange_kernel, outer, inner, elems, ch...  49.9 us
    pallas_call x1, Pallas kernels, finish(): pl.pallas_call(functools.partial(finish_kernel, outer, inner, per_step),...  18 us
    unnamed x4, local copies, waits for them, and re-layouts  3.48 us

commit v1 on v0

v1 whole, which is shorter than its diff:
```python
import functools

import jax
import jax.numpy as jnp
import numpy as np
from jax import lax
from jax.experimental import pallas as pl
from jax.experimental.pallas import tpu as pltpu
from jax.sharding import PartitionSpec as P

GLL_POINTS = np.array(
    [
        -1.0,
        -0.8717401485096066,
        -0.5917001814331423,
        -0.2092992179024789,
        0.2092992179024789,
        0.5917001814331423,
        0.8717401485096066,
        1.0,
    ]
)
F32, BF16, I32, I16 = jnp.float32, jnp.bfloat16, jnp.int32, jnp.int16
MESH = pl.DeviceIdType.MESH
LANES = 128
GROUPS = 32
PICK_ROWS = 512
FACE_CHUNKS = 4


def lagrange_constants():
    table = np.zeros((8, 8, LANES))
    for i in range(8):
        table[0, i] = 1.0 / np.prod([GLL_POINTS[i] - GLL_POINTS[m] for m in range(8) if m != i])
        for r in range(1, 8):
            table[r, i] = GLL_POINTS[(i + r) % 8]
    return table.astype(np.float32)


def face_selector():
    cube = np.arange(512).reshape(8, 8, 8)
    faces = [cube[0], cube[7], cube[:, 0], cube[:, 7], cube[:, :, 0], cube[:, :, 7]]
    nodes = np.concatenate([face.reshape(-1) for face in faces])
    return (np.arange(512)[:, None] == nodes[None, :]).astype(np.float32)


def round_up(x, to):
    return -(-x // to) * to


def split2(x):
    hi = x.astype(BF16).astype(F32)
    return hi, x - hi


def dot(a, b):
    return lax.dot_general(a, b, (((1,), (0,)), ((), ())), preferred_element_type=F32)


def dot_nt(a, b):
    return lax.dot_general(a, b, (((1,), (1,)), ((), ())), preferred_element_type=F32)


def rows16(row):
    return jnp.broadcast_to(row, (16, row.shape[1])).astype(I16)


def stack(tile, count):
    return jnp.concatenate([tile] * count, axis=0)


def bounded(index, most):
    return jnp.minimum(jnp.maximum(index, 0), most)


def split_position(pos, size):
    group = jnp.floor((pos + 0.5) * (1.0 / size))
    return group, pos - group * size


def positions(peers, tiles_each, code_base, owner_ref, tri_ref, low_ref, pos_ref, meta_ref):
    rows = owner_ref.shape[0]
    wide = meta_ref.shape[1] - LANES
    batch = 8
    owner = owner_ref[...]
    lane = lax.broadcasted_iota(I32, (1, LANES), 1)
    tile_at = lax.broadcasted_iota(I32, (1, wide), 1).astype(F32)

    def step(it, state):
        pos, first, starts, code = state
        hots = [owner == it * batch + q for q in range(batch)]
        ones = jnp.concatenate([jnp.where(hot, 1.0, 0.0) for hot in hots], axis=0).astype(BF16)
        counted = dot(ones, tri_ref[...])
        counts = [counted[rows * q : rows * (q + 1), LANES:] for q in range(batch)]
        before = dot(low_ref[...], jnp.concatenate(counts, axis=1).astype(BF16))
        for q in range(batch):
            earlier = before[:, LANES * q : LANES * (q + 1)]
            slot = counted[rows * q : rows * (q + 1), :LANES] + earlier
            pos = jnp.where(hots[q], slot + (first * LANES - 1.0), pos)
            number = earlier[rows - 1 :] + counts[q][rows - 1 :]
            starts = jnp.where(lane == it * batch + q, first, starts)
            begin = jnp.concatenate([first] * (wide // LANES), axis=1)
            here = code_base(it * batch + q).astype(F32) + jnp.minimum(tile_at - begin, tiles_each - 1.0)
            code = jnp.where(tile_at >= begin, here, code)
            first = first + jnp.floor((number + (LANES - 1.0)) * (1.0 / LANES))
        return pos, first, starts, code

    zero = jnp.zeros((1, LANES), F32)
    state = (jnp.zeros(owner.shape, F32), zero, zero, jnp.zeros((1, wide), F32))
    for it in range(peers // batch):
        state = step(it, state)
    pos, _, starts, code = state
    pos_ref[...] = pos
    meta_ref[...] = jnp.concatenate([starts, code], axis=1).astype(I32)


def place(span, begin, end, pos_ref, coords_ref, elem_ref, row_ref, group_ref, acc):
    size = acc.shape[0]
    wide = group_ref.shape[0]

    @pl.loop(begin, end)
    def _(it):
        hots, spreads = [], []
        for r in range(span):
            row = it * span + r
            group, at = split_position(pos_ref[pl.ds(row, 1), :], size)
            at = stack(rows16(at.astype(I32)), size // 16)
            hots.append(jnp.where(row_ref[0:size, :] == at, jnp.array(1, BF16), jnp.array(0, BF16)))
            lanes = pl.ds(pl.multiple_of(row * LANES, LANES), LANES)
            hi, lo = split2(coords_ref[:, lanes])
            elem = elem_ref[pl.ds(row, 1), :].astype(F32)
            values = jnp.concatenate([hi, elem, lo, jnp.zeros((1, LANES), F32)], axis=0)
            values = stack(stack(values, 2).astype(BF16), wide // 16)
            group = stack(rows16(group.astype(I32)), wide // 16)
            spreads.append(jnp.where(group_ref[...] == group, values, jnp.array(0, BF16)))
        acc[...] += dot_nt(jnp.concatenate(hots, axis=1), jnp.concatenate(spreads, axis=1))


def interpolate(elems, load, store, tiles, chunk, stacked, lag_ref, elem_rows):
    per = chunk // LANES
    for at in range(0, tiles, per):
        x = jnp.concatenate([load(at + t) for t in range(per)], axis=1)
        weights = []
        for d in range(3):
            coord = jnp.broadcast_to(x[d : d + 1], (8, chunk))
            const = [jnp.concatenate([lag_ref[r]] * per, axis=1) for r in range(8)]
            w = const[0] * (coord - const[1])
            for r in range(2, 8):
                w = w * (coord - const[r])
            weights.append(w)
        elem = stack(rows16(x[3:4].astype(I32)), elems // 16)
        pick = jnp.concatenate([elem_rows] * per, axis=1) == elem
        parts = []
        for part in split2(weights[0]):
            pieces = []
            for parity in range(2):
                for m in range(4):
                    i = 2 * m + parity
                    row = stack(jnp.broadcast_to(part[i : i + 1], (16, chunk)).astype(BF16), elems // 16)
                    pieces.append(jnp.where(pick, row, jnp.array(0, BF16)))
            parts.append(jnp.concatenate(pieces, axis=0))
        a_hi, a_lo = parts
        summed = dot(stacked[...], jnp.concatenate([a_hi, a_lo, a_hi], axis=0))
        results = []
        for c in range(3):
            total = None
            for j in range(8):
                term = summed[64 * c + 8 * j : 64 * c + 8 * j + 8] * weights[1][j : j + 1]
                total = term if total is None else total + term
            results.append(jnp.sum(total * weights[2], axis=0, keepdims=True))
        result = jnp.concatenate(results, axis=0)
        for t in range(per):
            store(at + t, result[:, LANES * t : LANES * (t + 1)])


def advect_kernel(
    outer, inner, tiles_each, sorted_tiles, chunk,
    vel_ref, coords_ref, owner_ref, elem_ref, nb_ref, tri_ref, low_ref, lag_ref, sel_ref, sel_t_ref,
    out_ref,
    pos_ref, meta_ref, meta_smem, row_ref, group_ref, acc, sorted_ref, send_ref, table_ref, mirror_ref,
    stacked, arrived, replies, landed, answers, halves, vals, faces, below, above,
    meta_sem, table_out, table_in, go_out, go_in, back_out, back_in, face_out, face_in,
):
    peers = outer * inner
    hin = inner // 2
    half = peers // 2
    elems = vel_ref.shape[1]
    points = coords_ref.shape[1]
    size = acc.shape[0]
    my_x, my_y = lax.axis_index("gx"), lax.axis_index("gy")
    side, low_y = my_y // hin, lax.rem(my_y, hin)
    me = my_x * inner + my_y
    mine = my_x * hin + low_y
    barrier = pltpu.get_barrier_semaphore()

    def place_of(device):
        return (device // inner, lax.rem(device, inner))

    @pl.loop(1, peers)
    def _(s):
        pl.semaphore_signal(barrier, inc=1, device_id=place_of(lax.rem(me + s, peers)), device_id_type=MESH)

    def code_base(p):
        x, y = p // inner, p % inner
        w = lax.rem(y // hin + side, 2)
        return (w * half + x * hin + y % hin) * tiles_each

    positions(peers, tiles_each, code_base, owner_ref, tri_ref, low_ref, pos_ref, meta_ref)
    meta_copy = pltpu.make_async_copy(meta_ref, meta_smem, meta_sem)
    meta_copy.start()

    row_ref[...] = lax.broadcasted_iota(I32, row_ref.shape, 0).astype(I16)
    group_ref[...] = (lax.broadcasted_iota(I32, group_ref.shape, 0) // 8).astype(I16)
    acc[...] = jnp.zeros_like(acc)
    for c in range(3):
        cube = vel_ref[c]
        tall = jnp.concatenate([cube[:, LANES * m : LANES * (m + 1)] for m in range(4)], axis=0).T
        table_ref[64 * c : 64 * (c + 1)] = jnp.concatenate([tall[0:64], tall[64:128]], axis=1)

    span = 8
    steps = points // LANES // span
    place(span, 0, steps // 2, pos_ref, coords_ref, elem_ref, row_ref, group_ref, acc)
    pl.semaphore_wait(barrier, peers - 1)
    table_copy = pltpu.make_async_remote_copy(
        src_ref=table_ref, dst_ref=mirror_ref, send_sem=table_out, recv_sem=table_in,
        device_id=(my_x, lax.rem(my_y + hin, inner)), device_id_type=MESH,
    )
    table_copy.start()
    place(span, steps // 2, steps, pos_ref, coords_ref, elem_ref, row_ref, group_ref, acc)

    per_group = size // LANES
    for j in range(per_group):
        turned = acc[LANES * j : LANES * (j + 1), :].T
        for g in range(GROUPS):
            sorted_ref[g * per_group + j] = turned[8 * g : 8 * g + 8]
    for t in range(GROUPS * per_group, sorted_tiles):
        sorted_ref[t] = jnp.zeros((8, LANES), F32)

    def after(s):
        x, y = lax.rem(my_x + lax.rem(s, outer), outer), lax.rem(low_y + s // outer, hin)
        return x, y

    def before(s):
        x = lax.rem(my_x + outer - lax.rem(s, outer), outer)
        y = lax.rem(low_y + hin - s // outer, hin)
        return x, y

    def block(w, device):
        return pl.ds((w * half + device) * tiles_each, tiles_each)

    def outgoing(w, s, place_at):
        x, y = place_at(s)
        device = x * hin + y
        return device, pltpu.make_async_remote_copy(
            src_ref=send_ref.at[block(w, device)], dst_ref=arrived.at[block(w, mine)],
            send_sem=go_out.at[w, device], recv_sem=go_in.at[w, mine],
            device_id=(x, y + side * hin), device_id_type=MESH,
        )

    def incoming(w, s):
        x, y = before(s)
        device = x * hin + y
        return device, pltpu.make_async_remote_copy(
            src_ref=send_ref.at[block(w, device)], dst_ref=arrived.at[block(w, device)],
            send_sem=go_out.at[w, device], recv_sem=go_in.at[w, device],
            device_id=(x, y + side * hin), device_id_type=MESH,
        )

    def reply(w, s):
        x, y = before(s)
        device = x * hin + y
        return pltpu.make_async_remote_copy(
            src_ref=replies.at[block(w, device)], dst_ref=landed.at[block(w, mine)],
            send_sem=back_out.at[w, device], recv_sem=back_in.at[w, mine],
            device_id=(x, y + side * hin), device_id_type=MESH,
        )

    def answer(w, s):
        x, y = after(s)
        device = x * hin + y
        return pltpu.make_async_remote_copy(
            src_ref=replies.at[block(w, device)], dst_ref=landed.at[block(w, device)],
            send_sem=back_out.at[w, device], recv_sem=back_in.at[w, device],
            device_id=(x, y + side * hin), device_id_type=MESH,
        )

    meta_copy.wait()

    def pack(w, s):
        x, y = after(s)
        owner = x * inner + y + lax.rem(side + w, 2) * hin
        first = bounded(meta_smem[0, owner], sorted_tiles - tiles_each)
        base = (w * half + x * hin + y) * tiles_each
        for k in range(tiles_each):
            send_ref[base + k] = sorted_ref[first + k, 0:4, :] + sorted_ref[first + k, 4:8, :]

    for w in range(2):
        @pl.loop(1, half)
        def _(s):
            pack(w, s)
            outgoing(w, s, after)[1].start()

        pack(w, 0)

    elem_rows = row_ref[0:elems, :]
    for w in range(2):
        if w == 1:
            table_copy.wait_recv()
        hi, lo = split2(table_ref[...] if w == 0 else mirror_ref[...])
        stacked[...] = jnp.concatenate([hi, hi, lo], axis=1).astype(BF16)
        own = (w * half + mine) * tiles_each

        def own_store(t, value):
            landed[own + t, 0:3, :] = value

        interpolate(elems, lambda t: send_ref[own + t], own_store, tiles_each, chunk, stacked, lag_ref, elem_rows)

        @pl.loop(1, half)
        def _(s):
            device, copy = incoming(w, s)
            copy.wait_recv()
            base = (w * half + device) * tiles_each

            def store(t, value):
                replies[base + t, 0:3, :] = value

            interpolate(elems, lambda t: arrived[base + t], store, tiles_each, chunk, stacked, lag_ref, elem_rows)
            reply(w, s).start()

    table_copy.wait_send()
    for w in range(2):
        @pl.loop(1, half)
        def _(s):
            answer(w, s).wait_recv()

    groups = answers.shape[0]
    per_row = PICK_ROWS // LANES
    for g in range(groups):
        for j in range(per_row):
            answers[g, :, LANES * j : LANES * (j + 1)] = landed[
                bounded(meta_smem[0, LANES + g * per_row + j], landed.shape[0] - 1)
            ]
    for c in range(3):
        hi, lo = split2(answers[:, c, :])
        halves[groups * c : groups * (c + 1)] = hi.astype(BF16)
        halves[groups * (c + 3) : groups * (c + 4)] = lo.astype(BF16)

    up, down = lax.rem(me + 1, peers), lax.rem(me + peers - 1, peers)
    face_elems = elems // FACE_CHUNKS
    group_iota = lax.broadcasted_iota(I32, (groups, 512), 0).astype(F32)
    copies = []
    for q in range(FACE_CHUNKS):
        @pl.loop(0, face_elems)
        def _(k):
            e = q * face_elems + k
            pos = jnp.concatenate([pos_ref[pl.ds(4 * e + r, 1), :] for r in range(4)], axis=1)
            group, at = split_position(pos, PICK_ROWS)
            at = stack(rows16(at.astype(I32)), PICK_ROWS // 16)
            rows = jnp.concatenate([row_ref[0:PICK_ROWS, :]] * 4, axis=1)
            picked = dot(halves[...], jnp.where(rows == at, jnp.array(1, BF16), jnp.array(0, BF16)))
            match = group_iota == group
            for c in range(3):
                both = picked[groups * c : groups * (c + 1)] + picked[groups * (c + 3) : groups * (c + 4)]
                vals[c, pl.ds(e, 1), :] = jnp.sum(jnp.where(match, both, 0.0), axis=0, keepdims=True)

        some = slice(q * face_elems, (q + 1) * face_elems)
        hi, lo = split2(jnp.concatenate([vals[c, some, :] for c in range(3)], axis=0))
        both = dot(jnp.concatenate([hi, lo], axis=0).astype(BF16), sel_ref[...])
        both = both[0 : 3 * face_elems] + both[3 * face_elems :]
        for c in range(3):
            faces[q, c] = both[face_elems * c : face_elems * (c + 1)]
        for k, (device, land) in enumerate(((up, below), (down, above))):
            copy = pltpu.make_async_remote_copy(
                src_ref=faces.at[q], dst_ref=land.at[q],
                send_sem=face_out.at[q, k], recv_sem=face_in.at[q, k],
                device_id=place_of(device), device_id_type=MESH,
            )
            copy.start()
            copies.append(copy)

    index = (nb_ref[...] - jnp.where(nb_ref[...] >= 0, (me - 1) * elems, 0)).astype(F32)
    index = jnp.concatenate([index, jnp.zeros((2, elems), F32)], axis=0)
    index = jnp.concatenate([index] * (LANES // elems), axis=1).T[0:elems]
    columns = lax.broadcasted_iota(I32, (elems, 3 * elems), 1).astype(F32)
    column = [jnp.broadcast_to(index[:, f : f + 1], (elems, 3 * elems)) for f in range(6)]
    picker = jnp.concatenate([jnp.where(columns == column[f], 1.0, 0.0) for f in range(6)], axis=0).astype(BF16)
    present = [jnp.where(index[:, f : f + 1] >= 0, 0.5, 0.0) for f in range(6)]

    for w in range(2):
        @pl.loop(1, half)
        def _(s):
            outgoing(w, s, after)[1].wait_send()
            reply(w, s).wait_send()

    for copy in copies:
        copy.wait()

    def whole(ref, c):
        return jnp.concatenate([ref[q, c] for q in range(FACE_CHUNKS)], axis=0)

    changes = []
    for c in range(3):
        own = whole(faces, c)
        extended = jnp.concatenate([whole(below, c), own, whole(above, c)], axis=0)
        hi, lo = split2(extended)
        across = dot(picker, hi.astype(BF16)) + dot(picker, lo.astype(BF16))
        pieces = []
        for f in range(6):
            g = f ^ 1
            rows = slice(f * elems, (f + 1) * elems)
            other = across[rows, 64 * g : 64 * g + 64]
            pieces.append(0.5 * other - present[f] * own[:, 64 * f : 64 * f + 64])
        changes.append(jnp.concatenate(pieces, axis=1))
    hi, lo = split2(jnp.concatenate(changes, axis=0))
    spread = dot(jnp.concatenate([hi, lo], axis=0).astype(BF16), sel_t_ref[...])
    for c in range(3):
        rows = slice(c * elems, (c + 1) * elems)
        out_ref[c] = vals[c] + (spread[rows] + spread[(c + 3) * elems : (c + 4) * elems])


def advect(velocity, coords, owner, elem, neighbours, outer, inner):
    peers = outer * inner
    half = peers // 2
    elems = velocity.shape[1]
    points = coords.shape[1]
    capacity = 2 * points // peers
    tiles_each = capacity // LANES
    used = round_up(points // LANES + peers, GROUPS)
    size = used // GROUPS * LANES
    sorted_tiles = used + tiles_each
    groups = round_up(used * LANES, PICK_ROWS * 8) // PICK_ROWS
    code_lanes = round_up(groups * PICK_ROWS // LANES, LANES)
    tri = np.concatenate([np.triu(np.ones((LANES, LANES))), np.ones((LANES, LANES))], axis=1)
    low = np.tril(np.ones((points // LANES, points // LANES)), -1)
    sel = face_selector()
    face_block = (FACE_CHUNKS, 3, elems // FACE_CHUNKS, 384)
    vmem = pl.BlockSpec(memory_space=pltpu.VMEM)
    return pl.pallas_call(
        functools.partial(advect_kernel, outer, inner, tiles_each, sorted_tiles, min(capacity, 256)),
        in_specs=[vmem] * 10,
        out_specs=vmem,
        out_shape=jax.ShapeDtypeStruct((3, elems, 512), F32),
        scratch_shapes=[
            pltpu.VMEM((points // LANES, LANES), F32),
            pltpu.VMEM((1, LANES + code_lanes), I32),
            pltpu.SMEM((1, LANES + code_lanes), I32),
            pltpu.VMEM((max(size, PICK_ROWS), LANES), I16),
            pltpu.VMEM((GROUPS * 8, LANES), I16),
            pltpu.VMEM((size, GROUPS * 8), F32),
            pltpu.VMEM((sorted_tiles, 8, LANES), F32),
            pltpu.VMEM((peers * tiles_each, 4, LANES), F32),
            pltpu.VMEM((192, elems * 8), F32),
            pltpu.VMEM((192, elems * 8), F32),
            pltpu.VMEM((192, 3 * elems * 8), BF16),
            pltpu.VMEM((peers * tiles_each, 4, LANES), F32),
            pltpu.VMEM((peers * tiles_each, 4, LANES), F32),
            pltpu.VMEM((peers * tiles_each, 4, LANES), F32),
            pltpu.VMEM((groups, 4, PICK_ROWS), F32),
            pltpu.VMEM((6 * groups, PICK_ROWS), BF16),
            pltpu.VMEM((3, elems, 512), F32),
            pltpu.VMEM(face_block, F32),
            pltpu.VMEM(face_block, F32),
            pltpu.VMEM(face_block, F32),
            pltpu.SemaphoreType.DMA,
            pltpu.SemaphoreType.DMA,
            pltpu.SemaphoreType.DMA,
        ]
        + [pltpu.SemaphoreType.DMA((2, half))] * 4
        + [pltpu.SemaphoreType.DMA((FACE_CHUNKS, 2))] * 2,
        compiler_params=pltpu.CompilerParams(collective_id=0, has_side_effects=True),
        name="advect",
    )(
        velocity, coords, owner, elem, neighbours, jnp.asarray(tri, BF16), jnp.asarray(low, BF16),
        jnp.asarray(lagrange_constants()), jnp.asarray(sel, BF16), jnp.asarray(sel.T, BF16),
    )


def local(velocity, depart, owner_rank, owner_element_index, neighbours):
    outer, inner = lax.axis_size("gx"), lax.axis_size("gy")
    rows = depart.shape[1] // LANES
    owner = owner_rank.reshape(rows, LANES)
    elem = owner_element_index.reshape(rows, LANES)
    return advect(velocity, depart, owner, elem, neighbours, outer, inner)


def solution(mesh):
    placed = (
        P(None, ("gx", "gy"), None),
        P(None, ("gx", "gy")),
        P(("gx", "gy"), None),
        P(("gx", "gy")),
        P(None, ("gx", "gy")),
    )
    return jax.shard_map(
        local, mesh=mesh, in_specs=placed, out_specs=P(None, ("gx", "gy"), None), check_vma=False
    )
```

time: 74.2 us -> 61 us (0.82)
  Pallas kernels: 67.9 us -> 59.2 us
  local copies, waits for them, and re-layouts: 6.01 us -> 1.62 us
    pallas_call x2 -> x1, Pallas kernels: 67.9 us -> 59.2 us  [advect(): pl.pallas_call(functools.partial(advect_kernel, outer, inner, tiles_each,...]
    reshape x3 -> x0, local copies, waits for them, and re-layouts: 1.87 us -> none  [the longest x2 1.11 us: local(): velocity.reshape(3, elems, 64, 8).transpose(0, 2, 1, 3)]
    unnamed x4 -> x1, local copies, waits for them, and re-layouts: 3.48 us -> 1.62 us
where the time goes in v1:
time: 61 us; the launch traced here: 60.8 us
  Pallas kernels  59.2 us (97%)
  local copies, waits for them, and re-layouts  1.62 us (3%)
    pallas_call x1, Pallas kernels, advect(): pl.pallas_call(functools.partial(advect_kernel, outer, inner, tiles_each,...  59.2 us
    unnamed x1, local copies, waits for them, and re-layouts  1.62 us

profile of v1, /device:TPU:0, one launch (start us, length us, event | category | flops | bytes accessed | tf_op | source)
XLA Modules:
  0.0 60.8 jit_solution(5990549486104906271)
XLA Ops:
  0.0 59.2 %advect.1 = f32[3,32,512]{2,1,0:T(8,128)} custom-call(f32[3,32,512]{2,1,0:T(8,128)} %vel_ref.1, f32[3,16384]{1,0:T(4,128)} %coords_ref.1, s32[128,128]{1,0:T(8,128)} %bitcast.2, s32[128,128]{1,0:T(8,128)} %bitcast.3, s32[6,32]{1,0:T(8,128)} %nb_ref.1, bf16[128,256]{1,0:T(8,128)(2,1)} %constant.10.clone.tri_ref, bf16[128,128]{1,0:T(8,128)(2,1)} %constant.11.clone.low_ref, ...), custom_call_target="tpu_custom_call" | custom-call | tf_op jit(solution)/shard_map/advect/pallas_call | solution.py:438
  59.2 1.6 %copy.12 = f32[3,32,512]{2,1,0:T(8,128)} copy(f32[3,32,512]{2,1,0:T(8,128)} %advect.1) | data formatting | bytes 393216

commit v2 on v1

--- a/solution.py
+++ b/solution.py
@@ -44,6 +44,17 @@
     return (np.arange(512)[:, None] == nodes[None, :]).astype(np.float32)
 
 
+def node_split():
+    sel = face_selector()
+    first = sel * (np.cumsum(sel, axis=1) == 1)
+    inside = np.flatnonzero(sel.sum(axis=1) == 0)
+    rest = np.zeros((512, round_up(len(inside), LANES)), np.float32)
+    rest[inside, np.arange(len(inside))] = 1
+    order = np.concatenate([sel, rest], axis=1)
+    back = np.concatenate([first, rest], axis=1).T
+    return order, back, sel.T
+
+
 def round_up(x, to):
     return -(-x // to) * to
 
@@ -81,7 +92,7 @@
 def positions(peers, tiles_each, code_base, owner_ref, tri_ref, low_ref, pos_ref, meta_ref):
     rows = owner_ref.shape[0]
     wide = meta_ref.shape[1] - LANES
-    batch = 8
+    batch = min(peers, 32)
     owner = owner_ref[...]
     lane = lax.broadcasted_iota(I32, (1, LANES), 1)
     tile_at = lax.broadcasted_iota(I32, (1, wide), 1).astype(F32)
@@ -160,7 +171,8 @@
                     pieces.append(jnp.where(pick, row, jnp.array(0, BF16)))
             parts.append(jnp.concatenate(pieces, axis=0))
         a_hi, a_lo = parts
-        summed = dot(stacked[...], jnp.concatenate([a_hi, a_lo, a_hi], axis=0))
+        both = dot(stacked[...], a_hi)
+        summed = both[0:192] + both[192:384] + dot(stacked[0:192], a_lo)
         results = []
         for c in range(3):
             total = None
@@ -175,10 +187,11 @@
 
 def advect_kernel(
     outer, inner, tiles_each, sorted_tiles, chunk,
-    vel_ref, coords_ref, owner_ref, elem_ref, nb_ref, tri_ref, low_ref, lag_ref, sel_ref, sel_t_ref,
+    vel_ref, coords_ref, owner_ref, elem_ref, nb_ref, tri_ref, low_ref, lag_ref, order_ref, back_ref, sel_t_ref,
     out_ref,
     pos_ref, meta_ref, meta_smem, row_ref, group_ref, acc, sorted_ref, send_ref, table_ref, mirror_ref,
     stacked, arrived, replies, landed, answers, halves, vals, faces, below, above,
+    at_ref, group_of_ref, inner_ref,
     meta_sem, table_out, table_in, go_out, go_in, back_out, back_in, face_out, face_in,
 ):
     peers = outer * inner
@@ -217,16 +230,23 @@
         tall = jnp.concatenate([cube[:, LANES * m : LANES * (m + 1)] for m in range(4)], axis=0).T
         table_ref[64 * c : 64 * (c + 1)] = jnp.concatenate([tall[0:64], tall[64:128]], axis=1)
 
-    span = 8
+
+    def halve(w, table):
+        hi, lo = split2(table[...])
+        stacked[w] = jnp.concatenate([hi, lo], axis=0).astype(BF16)
+
+    halve(0, table_ref)
+
+    span = 32
     steps = points // LANES // span
-    place(span, 0, steps // 2, pos_ref, coords_ref, elem_ref, row_ref, group_ref, acc)
+    place(span, 0, steps // 4, pos_ref, coords_ref, elem_ref, row_ref, group_ref, acc)
     pl.semaphore_wait(barrier, peers - 1)
     table_copy = pltpu.make_async_remote_copy(
         src_ref=table_ref, dst_ref=mirror_ref, send_sem=table_out, recv_sem=table_in,
         device_id=(my_x, lax.rem(my_y + hin, inner)), device_id_type=MESH,
     )
     table_copy.start()
-    place(span, steps // 2, steps, pos_ref, coords_ref, elem_ref, row_ref, group_ref, acc)
+    place(span, steps // 4, steps, pos_ref, coords_ref, elem_ref, row_ref, group_ref, acc)
 
     per_group = size // LANES
     for j in range(per_group):
@@ -236,96 +256,104 @@
     for t in range(GROUPS * per_group, sorted_tiles):
         sorted_ref[t] = jnp.zeros((8, LANES), F32)
 
-    def after(s):
-        x, y = lax.rem(my_x + lax.rem(s, outer), outer), lax.rem(low_y + s // outer, hin)
-        return x, y
-
-    def before(s):
-        x = lax.rem(my_x + outer - lax.rem(s, outer), outer)
-        y = lax.rem(low_y + hin - s // outer, hin)
-        return x, y
+    def partner(s):
+        device = mine ^ s
+        return device, (device // hin, lax.rem(device, hin) + side * hin)
 
     def block(w, device):
         return pl.ds((w * half + device) * tiles_each, tiles_each)
 
-    def outgoing(w, s, place_at):
-        x, y = place_at(s)
-        device = x * hin + y
-        return device, pltpu.make_async_remote_copy(
-            src_ref=send_ref.at[block(w, device)], dst_ref=arrived.at[block(w, mine)],
-            send_sem=go_out.at[w, device], recv_sem=go_in.at[w, mine],
-            device_id=(x, y + side * hin), device_id_type=MESH,
+    def remote(src, dst, out_sem, in_sem, w, s):
+        device, where = partner(s)
+        return pltpu.make_async_remote_copy(
+            src_ref=src.at[block(w, device)], dst_ref=dst.at[block(w, mine)],
+            send_sem=out_sem.at[w, device], recv_sem=in_sem.at[w, mine],
+            device_id=where, device_id_type=MESH,
         )
 
-    def incoming(w, s):
-        x, y = before(s)
-        device = x * hin + y
-        return device, pltpu.make_async_remote_copy(
-            src_ref=send_ref.at[block(w, device)], dst_ref=arrived.at[block(w, device)],
-            send_sem=go_out.at[w, device], recv_sem=go_in.at[w, device],
-            device_id=(x, y + side * hin), device_id_type=MESH,
+    def arrival(src, dst, out_sem, in_sem, w, s):
+        device, where = partner(s)
+        return pltpu.make_async_remote_copy(
+            src_ref=src.at[block(w, device)], dst_ref=dst.at[block(w, device)],
+            send_sem=out_sem.at[w, device], recv_sem=in_sem.at[w, device],
+            device_id=where, device_id_type=MESH,
         )
 
-    def reply(w, s):
-        x, y = before(s)
-        device = x * hin + y
-        return pltpu.make_async_remote_copy(
-            src_ref=replies.at[block(w, device)], dst_ref=landed.at[block(w, mine)],
-            send_sem=back_out.at[w, device], recv_sem=back_in.at[w, mine],
-            device_id=(x, y + side * hin), device_id_type=MESH,
-        )
-
-    def answer(w, s):
-        x, y = after(s)
-        device = x * hin + y
-        return pltpu.make_async_remote_copy(
-            src_ref=replies.at[block(w, device)], dst_ref=landed.at[block(w, device)],
-            send_sem=back_out.at[w, device], recv_sem=back_in.at[w, device],
-            device_id=(x, y + side * hin), device_id_type=MESH,
-        )
+    outgoing = functools.partial(remote, send_ref, arrived, go_out, go_in)
+    incoming = functools.partial(arrival, send_ref, arrived, go_out, go_in)
+    reply = functools.partial(remote, replies, landed, back_out, back_in)
+    answer = functools.partial(arrival, replies, landed, back_out, back_in)
 
     meta_copy.wait()
 
-    def pack(w, s):
-        x, y = after(s)
-        owner = x * inner + y + lax.rem(side + w, 2) * hin
+    def pack(into, w, s):
+        device = mine ^ s
+        owner = device // hin * inner + lax.rem(device, hin) + lax.rem(side + w, 2) * hin
         first = bounded(meta_smem[0, owner], sorted_tiles - tiles_each)
-        base = (w * half + x * hin + y) * tiles_each
+        base = (w * half + device) * tiles_each
         for k in range(tiles_each):
-            send_ref[base + k] = sorted_ref[first + k, 0:4, :] + sorted_ref[first + k, 4:8, :]
+            into[base + k] = sorted_ref[first + k, 0:4, :] + sorted_ref[first + k, 4:8, :]
+
+    def order(w, s):
+        return s if w == 0 else half - s
 
     for w in range(2):
         @pl.loop(1, half)
         def _(s):
-            pack(w, s)
-            outgoing(w, s, after)[1].start()
-
-        pack(w, 0)
+            pack(send_ref, w, order(w, s))
+            outgoing(w, order(w, s)).start()
+
+        pack(arrived, w, 0)
+
+    pos = jnp.concatenate([pos_ref[pl.ds(r, elems, stride=4), :] for r in range(4)], axis=1)
+    group, at = split_position(pos, PICK_ROWS)
+    at_high = jnp.floor(at * 0.5)
+    digits = jnp.concatenate([group, at_high, at - 2.0 * at_high], axis=0).astype(BF16)
+    digits = dot(digits, order_ref[...])
+    group_of_ref[...] = digits[0:elems].astype(I32)
+    at_ref[...] = (2.0 * digits[elems : 2 * elems] + digits[2 * elems :]).astype(I32)
 
     elem_rows = row_ref[0:elems, :]
-    for w in range(2):
-        if w == 1:
+    together = 4
+    turns = half // together
+
+    @pl.loop(0, 2 * turns)
+    def _(it):
+        w, turn = it // turns, lax.rem(it, turns)
+
+        @pl.when(it == turns)
+        def _():
             table_copy.wait_recv()
-        hi, lo = split2(table_ref[...] if w == 0 else mirror_ref[...])
-        stacked[...] = jnp.concatenate([hi, hi, lo], axis=1).astype(BF16)
-        own = (w * half + mine) * tiles_each
-
-        def own_store(t, value):
-            landed[own + t, 0:3, :] = value
-
-        interpolate(elems, lambda t: send_ref[own + t], own_store, tiles_each, chunk, stacked, lag_ref, elem_rows)
-
-        @pl.loop(1, half)
-        def _(s):
-            device, copy = incoming(w, s)
-            copy.wait_recv()
-            base = (w * half + device) * tiles_each
+            halve(1, mirror_ref)
+
+        sources = []
+        for u in range(together):
+            s = together * turn + u
+            s = s + w * (half - 1 - 2 * s)
+            sources.append(s)
+
+            @pl.when(s > 0)
+            def _():
+                incoming(w, s).wait_recv()
+
+        for s in sources:
+            base = (w * half + (mine ^ s)) * tiles_each
 
             def store(t, value):
                 replies[base + t, 0:3, :] = value
 
-            interpolate(elems, lambda t: arrived[base + t], store, tiles_each, chunk, stacked, lag_ref, elem_rows)
-            reply(w, s).start()
+            interpolate(
+                elems, lambda t: arrived[base + t], store, tiles_each, chunk, stacked.at[w], lag_ref, elem_rows
+            )
+        for s in sources:
+            @pl.when(s > 0)
+            def _():
+                reply(w, s).start()
+
+    for w in range(2):
+        own = (w * half + mine) * tiles_each
+        for t in range(tiles_each):
+            landed[own + t] = replies[own + t]
 
     table_copy.wait_send()
     for w in range(2):
@@ -333,50 +361,81 @@
         def _(s):
             answer(w, s).wait_recv()
 
-    groups = answers.shape[0]
+    groups = answers.shape[1] // 4
     per_row = PICK_ROWS // LANES
     for g in range(groups):
         for j in range(per_row):
-            answers[g, :, LANES * j : LANES * (j + 1)] = landed[
+            answers[j, 4 * g : 4 * g + 4, :] = landed[
                 bounded(meta_smem[0, LANES + g * per_row + j], landed.shape[0] - 1)
             ]
     for c in range(3):
-        hi, lo = split2(answers[:, c, :])
+        rows = [answers[j, pl.ds(c, groups, stride=4), :] for j in range(per_row)]
+        hi, lo = split2(jnp.concatenate(rows, axis=1))
         halves[groups * c : groups * (c + 1)] = hi.astype(BF16)
         halves[groups * (c + 3) : groups * (c + 4)] = lo.astype(BF16)
 
     up, down = lax.rem(me + 1, peers), lax.rem(me + peers - 1, peers)
     face_elems = elems // FACE_CHUNKS
-    group_iota = lax.broadcasted_iota(I32, (groups, 512), 0).astype(F32)
-    copies = []
-    for q in range(FACE_CHUNKS):
-        @pl.loop(0, face_elems)
-        def _(k):
-            e = q * face_elems + k
-            pos = jnp.concatenate([pos_ref[pl.ds(4 * e + r, 1), :] for r in range(4)], axis=1)
-            group, at = split_position(pos, PICK_ROWS)
-            at = stack(rows16(at.astype(I32)), PICK_ROWS // 16)
-            rows = jnp.concatenate([row_ref[0:PICK_ROWS, :]] * 4, axis=1)
-            picked = dot(halves[...], jnp.where(rows == at, jnp.array(1, BF16), jnp.array(0, BF16)))
-            match = group_iota == group
-            for c in range(3):
-                both = picked[groups * c : groups * (c + 1)] + picked[groups * (c + 3) : groups * (c + 4)]
-                vals[c, pl.ds(e, 1), :] = jnp.sum(jnp.where(match, both, 0.0), axis=0, keepdims=True)
-
-        some = slice(q * face_elems, (q + 1) * face_elems)
-        hi, lo = split2(jnp.concatenate([vals[c, some, :] for c in range(3)], axis=0))
-        both = dot(jnp.concatenate([hi, lo], axis=0).astype(BF16), sel_ref[...])
-        both = both[0 : 3 * face_elems] + both[3 * face_elems :]
+
+    def pick(first, count, begin, width, store):
+        def flat(ref):
+            return jnp.concatenate([ref[pl.ds(first + u, 1), begin : begin + width] for u in range(count)], axis=1)
+
+        at, group = flat(at_ref), flat(group_of_ref)
+        at = stack(rows16(at), PICK_ROWS // 16)
+        rows = jnp.concatenate([row_ref[0:PICK_ROWS, :]] * (count * width // LANES), axis=1)
+        picked = dot(halves[...], jnp.where(rows == at, jnp.array(1, BF16), jnp.array(0, BF16)))
+        match = lax.broadcasted_iota(I32, (groups, count * width), 0) == group
         for c in range(3):
-            faces[q, c] = both[face_elems * c : face_elems * (c + 1)]
-        for k, (device, land) in enumerate(((up, below), (down, above))):
-            copy = pltpu.make_async_remote_copy(
-                src_ref=faces.at[q], dst_ref=land.at[q],
-                send_sem=face_out.at[q, k], recv_sem=face_in.at[q, k],
-                device_id=place_of(device), device_id_type=MESH,
-            )
-            copy.start()
-            copies.append(copy)
+            both = picked[groups * c : groups * (c + 1)] + picked[groups * (c + 3) : groups * (c + 4)]
+            value = jnp.sum(jnp.where(match, both, 0.0), axis=0, keepdims=True)
+            for u in range(count):
+                store(c, u, value[:, width * u : width * (u + 1)])
+
+    def face_copy(q, k):
+        device, land = ((up, below), (down, above))[k]
+        return pltpu.make_async_remote_copy(
+            src_ref=faces.at[q], dst_ref=land.at[q],
+            send_sem=face_out.at[q, k], recv_sem=face_in.at[q, k],
+            device_id=place_of(device), device_id_type=MESH,
+        )
+
+    @pl.when(me == 0)
+    def _():
+        below[...] = jnp.zeros_like(below)
+
+    @pl.when(me == peers - 1)
+    def _():
+        above[...] = jnp.zeros_like(above)
+
+    step = 4
+    per_chunk = face_elems // step
+
+    @pl.loop(0, elems // step)
+    def _(it):
+        q, part = it // per_chunk, lax.rem(it, per_chunk)
+
+        def store(c, u, value):
+            faces[q, c, pl.ds(part * step + u, 1), :] = value
+
+        pick(it * step, step, 0, 384, store)
+
+        @pl.when((part == per_chunk - 1) & (me < peers - 1))
+        def _():
+            face_copy(q, 0).start()
+
+        @pl.when((part == per_chunk - 1) & (me > 0))
+        def _():
+            face_copy(q, 1).start()
+
+    inside = inner_ref.shape[2]
+
+    @pl.loop(0, elems // step)
+    def _(it):
+        def store(c, u, value):
+            inner_ref[c, pl.ds(it * step + u, 1), :] = value
+
+        pick(it * step, step, 384, inside, store)
 
     index = (nb_ref[...] - jnp.where(nb_ref[...] >= 0, (me - 1) * elems, 0)).astype(F32)
     index = jnp.concatenate([index, jnp.zeros((2, elems), F32)], axis=0)
@@ -389,33 +448,54 @@
     for w in range(2):
         @pl.loop(1, half)
         def _(s):
-            outgoing(w, s, after)[1].wait_send()
+            outgoing(w, s).wait_send()
             reply(w, s).wait_send()
-
-    for copy in copies:
-        copy.wait()
 
     def whole(ref, c):
         return jnp.concatenate([ref[q, c] for q in range(FACE_CHUNKS)], axis=0)
 
-    changes = []
-    for c in range(3):
-        own = whole(faces, c)
-        extended = jnp.concatenate([whole(below, c), own, whole(above, c)], axis=0)
-        hi, lo = split2(extended)
-        across = dot(picker, hi.astype(BF16)) + dot(picker, lo.astype(BF16))
-        pieces = []
-        for f in range(6):
-            g = f ^ 1
-            rows = slice(f * elems, (f + 1) * elems)
-            other = across[rows, 64 * g : 64 * g + 64]
-            pieces.append(0.5 * other - present[f] * own[:, 64 * f : 64 * f + 64])
-        changes.append(jnp.concatenate(pieces, axis=1))
-    hi, lo = split2(jnp.concatenate(changes, axis=0))
-    spread = dot(jnp.concatenate([hi, lo], axis=0).astype(BF16), sel_t_ref[...])
+    def halves_of(x):
+        hi, lo = split2(x)
+        return hi.astype(BF16), lo.astype(BF16)
+
+    def across_of(picks, parts):
+        hi, lo = halves_of(jnp.concatenate(parts, axis=1))
+        return dot(picks, hi) + dot(picks, lo)
+
+    def moved(across, c):
+        return jnp.concatenate(
+            [across[f * elems : (f + 1) * elems, 384 * c + 64 * (f ^ 1) : 384 * c + 64 * (f ^ 1) + 64] for f in range(6)],
+            axis=1,
+        )
+
+    own = [whole(faces, c) for c in range(3)]
+    present = jnp.concatenate([jnp.broadcast_to(p, (elems, 64)) for p in present], axis=1)
+    middle = across_of(picker[:, elems : 2 * elems], own)
+    base = [0.5 * moved(middle, c) - present * own[c] for c in range(3)]
+    kept = jnp.concatenate([jnp.concatenate([own[c], inner_ref[c]], axis=1) for c in range(3)], axis=0)
+    hi, lo = halves_of(kept)
+    spread = dot(jnp.concatenate([hi, lo], axis=0), back_ref[...])
+    vals[...] = spread[: 3 * elems] + spread[3 * elems :]
+
+    for q in range(FACE_CHUNKS):
+        @pl.when(me < peers - 1)
+        def _():
+            face_copy(q, 0).wait_send()
+            face_copy(q, 1).wait_recv()
+
+        @pl.when(me > 0)
+        def _():
+            face_copy(q, 1).wait_send()
+            face_copy(q, 0).wait_recv()
+
+    picks = jnp.concatenate([picker[:, :elems], picker[:, 2 * elems :]], axis=1)
+    outside = [jnp.concatenate([whole(below, c), whole(above, c)], axis=0) for c in range(3)]
+    outside = across_of(picks, outside)
+    hi, lo = halves_of(jnp.concatenate([base[c] + 0.5 * moved(outside, c) for c in range(3)], axis=0))
+    spread = dot(jnp.concatenate([hi, lo], axis=0), sel_t_ref[...])
     for c in range(3):
         rows = slice(c * elems, (c + 1) * elems)
-        out_ref[c] = vals[c] + (spread[rows] + spread[(c + 3) * elems : (c + 4) * elems])
+        out_ref[c] = vals[rows] + (spread[rows] + spread[(c + 3) * elems : (c + 4) * elems])
 
 
 def advect(velocity, coords, owner, elem, neighbours, outer, inner):
@@ -432,12 +512,12 @@
     code_lanes = round_up(groups * PICK_ROWS // LANES, LANES)
     tri = np.concatenate([np.triu(np.ones((LANES, LANES))), np.ones((LANES, LANES))], axis=1)
     low = np.tril(np.ones((points // LANES, points // LANES)), -1)
-    sel = face_selector()
+    order, back, sel_t = node_split()
     face_block = (FACE_CHUNKS, 3, elems // FACE_CHUNKS, 384)
     vmem = pl.BlockSpec(memory_space=pltpu.VMEM)
     return pl.pallas_call(
         functools.partial(advect_kernel, outer, inner, tiles_each, sorted_tiles, min(capacity, 256)),
-        in_specs=[vmem] * 10,
+        in_specs=[vmem] * 11,
         out_specs=vmem,
         out_shape=jax.ShapeDtypeStruct((3, elems, 512), F32),
         scratch_shapes=[
@@ -451,16 +531,19 @@
             pltpu.VMEM((peers * tiles_each, 4, LANES), F32),
             pltpu.VMEM((192, elems * 8), F32),
             pltpu.VMEM((192, elems * 8), F32),
-            pltpu.VMEM((192, 3 * elems * 8), BF16),
+            pltpu.VMEM((2, 384, elems * 8), BF16),
             pltpu.VMEM((peers * tiles_each, 4, LANES), F32),
             pltpu.VMEM((peers * tiles_each, 4, LANES), F32),
             pltpu.VMEM((peers * tiles_each, 4, LANES), F32),
-            pltpu.VMEM((groups, 4, PICK_ROWS), F32),
+            pltpu.VMEM((PICK_ROWS // LANES, 4 * groups, LANES), F32),
             pltpu.VMEM((6 * groups, PICK_ROWS), BF16),
-            pltpu.VMEM((3, elems, 512), F32),
+            pltpu.VMEM((3 * elems, 512), F32),
             pltpu.VMEM(face_block, F32),
             pltpu.VMEM(face_block, F32),
             pltpu.VMEM(face_block, F32),
+            pltpu.VMEM((elems, order.shape[1]), I32),
+            pltpu.VMEM((elems, order.shape[1]), I32),
+            pltpu.VMEM((3, elems, order.shape[1] - 384), F32),
             pltpu.SemaphoreType.DMA,
             pltpu.SemaphoreType.DMA,
             pltpu.SemaphoreType.DMA,
@@ -471,7 +554,8 @@
         name="advect",
     )(
         velocity, coords, owner, elem, neighbours, jnp.asarray(tri, BF16), jnp.asarray(low, BF16),
-        jnp.asarray(lagrange_constants()), jnp.asarray(sel, BF16), jnp.asarray(sel.T, BF16),
+        jnp.asarray(lagrange_constants()),
+        jnp.asarray(order, BF16), jnp.asarray(back, BF16), jnp.asarray(sel_t, BF16),
     )
 
 

time: 61 us -> 48.7 us (0.80)
  Pallas kernels: 59.2 us -> 46.9 us
    pallas_call x1, Pallas kernels: 59.2 us -> 46.9 us  [advect(): pl.pallas_call(functools.partial(advect_kernel, outer, inner, tiles_each,...]
where the time goes in v2:
time: 48.7 us; the launch traced here: 48.5 us
  Pallas kernels  46.9 us (96%)
  local copies, waits for them, and re-layouts  1.62 us (3%)
    pallas_call x1, Pallas kernels, advect(): pl.pallas_call(functools.partial(advect_kernel, outer, inner, tiles_each,...  46.9 us
    unnamed x1, local copies, waits for them, and re-layouts  1.62 us

profile of v2, /device:TPU:0, one launch (start us, length us, event | category | flops | bytes accessed | tf_op | source)
XLA Modules:
  0.0 48.5 jit_solution(16715501225380079704)
XLA Ops:
  0.0 46.9 %advect.1 = f32[3,32,512]{2,1,0:T(8,128)} custom-call(f32[3,32,512]{2,1,0:T(8,128)} %vel_ref.1, f32[3,16384]{1,0:T(4,128)} %coords_ref.1, s32[128,128]{1,0:T(8,128)} %bitcast.2, s32[128,128]{1,0:T(8,128)} %bitcast.3, s32[6,32]{1,0:T(8,128)} %nb_ref.1, bf16[128,256]{1,0:T(8,128)(2,1)} %constant.12.clone.tri_ref, bf16[128,128]{1,0:T(8,128)(2,1)} %constant.13.clone.low_ref, ...), custom_call_target="tpu_custom_call" | custom-call | tf_op jit(solution)/shard_map/advect/pallas_call | solution.py:518
  46.9 1.6 %copy.13 = f32[3,32,512]{2,1,0:T(8,128)} copy(f32[3,32,512]{2,1,0:T(8,128)} %advect.1) | data formatting | bytes 393216

commit v3 on v2

--- a/solution.py
+++ b/solution.py
@@ -51,8 +51,8 @@
     rest = np.zeros((512, round_up(len(inside), LANES)), np.float32)
     rest[inside, np.arange(len(inside))] = 1
     order = np.concatenate([sel, rest], axis=1)
-    back = np.concatenate([first, rest], axis=1).T
-    return order, back, sel.T
+    back = np.concatenate([first, rest, sel], axis=1).T
+    return order, back
 
 
 def round_up(x, to):
@@ -92,45 +92,37 @@
 def positions(peers, tiles_each, code_base, owner_ref, tri_ref, low_ref, pos_ref, meta_ref):
     rows = owner_ref.shape[0]
     wide = meta_ref.shape[1] - LANES
-    batch = min(peers, 32)
     owner = owner_ref[...]
     lane = lax.broadcasted_iota(I32, (1, LANES), 1)
     tile_at = lax.broadcasted_iota(I32, (1, wide), 1).astype(F32)
-
-    def step(it, state):
-        pos, first, starts, code = state
-        hots = [owner == it * batch + q for q in range(batch)]
-        ones = jnp.concatenate([jnp.where(hot, 1.0, 0.0) for hot in hots], axis=0).astype(BF16)
-        counted = dot(ones, tri_ref[...])
-        counts = [counted[rows * q : rows * (q + 1), LANES:] for q in range(batch)]
-        before = dot(low_ref[...], jnp.concatenate(counts, axis=1).astype(BF16))
-        for q in range(batch):
-            earlier = before[:, LANES * q : LANES * (q + 1)]
-            slot = counted[rows * q : rows * (q + 1), :LANES] + earlier
-            pos = jnp.where(hots[q], slot + (first * LANES - 1.0), pos)
-            number = earlier[rows - 1 :] + counts[q][rows - 1 :]
-            starts = jnp.where(lane == it * batch + q, first, starts)
-            begin = jnp.concatenate([first] * (wide // LANES), axis=1)
-            here = code_base(it * batch + q).astype(F32) + jnp.minimum(tile_at - begin, tiles_each - 1.0)
-            code = jnp.where(tile_at >= begin, here, code)
-            first = first + jnp.floor((number + (LANES - 1.0)) * (1.0 / LANES))
-        return pos, first, starts, code
-
-    zero = jnp.zeros((1, LANES), F32)
-    state = (jnp.zeros(owner.shape, F32), zero, zero, jnp.zeros((1, wide), F32))
-    for it in range(peers // batch):
-        state = step(it, state)
-    pos, _, starts, code = state
+    hots = [owner == p for p in range(peers)]
+    ones = jnp.concatenate([jnp.where(hot, 1.0, 0.0).astype(BF16) for hot in hots], axis=1)
+    ahead = dot(low_ref[...], ones)
+    columns = [ahead[rows - 1 :, LANES * p : LANES * (p + 1)] for p in range(peers)]
+    across = dot(jnp.concatenate(columns, axis=0).astype(BF16), tri_ref[...])
+    tiles = jnp.floor((across[:, LANES:] + (LANES - 1.0)) * (1.0 / LANES))
+    pos = jnp.zeros(owner.shape, F32)
+    first = jnp.zeros((1, LANES), F32)
+    starts, code = first, jnp.zeros((1, wide), F32)
+    for p in range(peers):
+        offset = across[p : p + 1, :LANES] + (first * LANES - 1.0)
+        pos = jnp.where(hots[p], ahead[:, LANES * p : LANES * (p + 1)] + offset, pos)
+        starts = jnp.where(lane == p, first, starts)
+        begin = jnp.concatenate([first] * (wide // LANES), axis=1)
+        here = code_base(p).astype(F32) + jnp.minimum(tile_at - begin, tiles_each - 1.0)
+        code = jnp.where(tile_at >= begin, here, code)
+        first = first + tiles[p : p + 1]
     pos_ref[...] = pos
     meta_ref[...] = jnp.concatenate([starts, code], axis=1).astype(I32)
 
 
-def place(span, begin, end, pos_ref, coords_ref, elem_ref, row_ref, group_ref, acc):
+def place(span, steps, ahead, pos_ref, coords_ref, elem_ref, row_ref, group_ref, acc):
     size = acc.shape[0]
     wide = group_ref.shape[0]
 
-    @pl.loop(begin, end)
+    @pl.loop(0, steps)
     def _(it):
+        ahead(it)
         hots, spreads = [], []
         for r in range(span):
             row = it * span + r
@@ -187,24 +179,39 @@
 
 def advect_kernel(
     outer, inner, tiles_each, sorted_tiles, chunk,
-    vel_ref, coords_ref, owner_ref, elem_ref, nb_ref, tri_ref, low_ref, lag_ref, order_ref, back_ref, sel_t_ref,
+    owner_hbm, tri_hbm, low_hbm, vel_hbm, coords_hbm, elem_hbm, nb_hbm, lag_hbm, order_hbm, back_hbm,
     out_ref,
+    owner_ref, tri_ref, low_ref, vel_ref, coords_ref, elem_ref, nb_ref, lag_ref, order_ref, back_ref,
+    load_sems,
     pos_ref, meta_ref, meta_smem, row_ref, group_ref, acc, sorted_ref, send_ref, table_ref, mirror_ref,
-    stacked, arrived, replies, landed, answers, halves, vals, faces, below, above,
-    at_ref, group_of_ref, inner_ref,
+    stacked, arrived, replies, landed, answers, halves, faces, below, above,
+    at_ref, group_of_ref, inner_ref, picker_ref, present_ref,
     meta_sem, table_out, table_in, go_out, go_in, back_out, back_in, face_out, face_in,
 ):
     peers = outer * inner
     hin = inner // 2
     half = peers // 2
-    elems = vel_ref.shape[1]
-    points = coords_ref.shape[1]
+    elems = vel_hbm.shape[1]
+    points = coords_hbm.shape[1]
     size = acc.shape[0]
     my_x, my_y = lax.axis_index("gx"), lax.axis_index("gy")
     side, low_y = my_y // hin, lax.rem(my_y, hin)
     me = my_x * inner + my_y
     mine = my_x * hin + low_y
     barrier = pltpu.get_barrier_semaphore()
+    loads = [
+        pltpu.make_async_copy(src, dst, load_sems.at[i])
+        for i, (src, dst) in enumerate((
+            (owner_hbm, owner_ref), (tri_hbm, tri_ref), (low_hbm, low_ref), (vel_hbm, vel_ref), (coords_hbm, coords_ref),
+            (elem_hbm, elem_ref), (nb_hbm, nb_ref), (lag_hbm, lag_ref), (order_hbm, order_ref), (back_hbm, back_ref),
+        ))
+    ]
+    for copy in loads:
+        copy.start()
+
+    def load(stage, count):
+        for copy in loads[stage : stage + count]:
+            copy.wait()
 
     def place_of(device):
         return (device // inner, lax.rem(device, inner))
@@ -213,11 +220,18 @@
     def _(s):
         pl.semaphore_signal(barrier, inc=1, device_id=place_of(lax.rem(me + s, peers)), device_id_type=MESH)
 
+    quarter = hin // 2
+
+    def mirror(y):
+        return (3 - y // quarter) * quarter + y % quarter
+
     def code_base(p):
         x, y = p // inner, p % inner
         w = lax.rem(y // hin + side, 2)
-        return (w * half + x * hin + y % hin) * tiles_each
-
+        low = y % hin + w * (mirror(y) % hin - y % hin)
+        return (w * half + x * hin + low) * tiles_each
+
+    load(0, 3)
     positions(peers, tiles_each, code_base, owner_ref, tri_ref, low_ref, pos_ref, meta_ref)
     meta_copy = pltpu.make_async_copy(meta_ref, meta_smem, meta_sem)
     meta_copy.start()
@@ -225,6 +239,7 @@
     row_ref[...] = lax.broadcasted_iota(I32, row_ref.shape, 0).astype(I16)
     group_ref[...] = (lax.broadcasted_iota(I32, group_ref.shape, 0) // 8).astype(I16)
     acc[...] = jnp.zeros_like(acc)
+    load(3, 1)
     for c in range(3):
         cube = vel_ref[c]
         tall = jnp.concatenate([cube[:, LANES * m : LANES * (m + 1)] for m in range(4)], axis=0).T
@@ -236,17 +251,31 @@
         stacked[w] = jnp.concatenate([hi, lo], axis=0).astype(BF16)
 
     halve(0, table_ref)
-
+    table_copy = pltpu.make_async_remote_copy(
+        src_ref=table_ref, dst_ref=mirror_ref, send_sem=table_out, recv_sem=table_in,
+        device_id=(my_x, (3 - my_y // quarter) * quarter + lax.rem(my_y, quarter)), device_id_type=MESH,
+    )
+    edge = my_y // quarter
+    outer_edge = (edge == 0) | (edge == 3)
+
+    load(4, 2)
     span = 32
     steps = points // LANES // span
-    place(span, 0, steps // 4, pos_ref, coords_ref, elem_ref, row_ref, group_ref, acc)
-    pl.semaphore_wait(barrier, peers - 1)
-    table_copy = pltpu.make_async_remote_copy(
-        src_ref=table_ref, dst_ref=mirror_ref, send_sem=table_out, recv_sem=table_in,
-        device_id=(my_x, lax.rem(my_y + hin, inner)), device_id_type=MESH,
-    )
-    table_copy.start()
-    place(span, steps // 4, steps, pos_ref, coords_ref, elem_ref, row_ref, group_ref, acc)
+
+    def ahead(it):
+        @pl.when(it == 1)
+        def _():
+            pl.semaphore_wait(barrier, peers - 1)
+
+        @pl.when((it == 1) & outer_edge)
+        def _():
+            table_copy.start()
+
+        @pl.when((it == steps - 1) & jnp.logical_not(outer_edge))
+        def _():
+            table_copy.start()
+
+    place(span, steps, ahead, pos_ref, coords_ref, elem_ref, row_ref, group_ref, acc)
 
     per_group = size // LANES
     for j in range(per_group):
@@ -288,7 +317,10 @@
 
     def pack(into, w, s):
         device = mine ^ s
-        owner = device // hin * inner + lax.rem(device, hin) + lax.rem(side + w, 2) * hin
+        y = lax.rem(device, hin) + side * hin
+        if w == 1:
+            y = (3 - y // quarter) * quarter + lax.rem(y, quarter)
+        owner = device // hin * inner + y
         first = bounded(meta_smem[0, owner], sorted_tiles - tiles_each)
         base = (w * half + device) * tiles_each
         for k in range(tiles_each):
@@ -298,13 +330,23 @@
         return s if w == 0 else half - s
 
     for w in range(2):
-        @pl.loop(1, half)
-        def _(s):
+        batch = 3
+
+        @pl.loop(0, (half - 1) // batch)
+        def _(it):
+            some = [order(w, 1 + it * batch + u) for u in range(batch)]
+            for s in some:
+                pack(send_ref, w, s)
+            for s in some:
+                outgoing(w, s).start()
+
+        for s in range(1 + (half - 1) // batch * batch, half):
             pack(send_ref, w, order(w, s))
             outgoing(w, order(w, s)).start()
 
         pack(arrived, w, 0)
 
+    load(6, 4)
     pos = jnp.concatenate([pos_ref[pl.ds(r, elems, stride=4), :] for r in range(4)], axis=1)
     group, at = split_position(pos, PICK_ROWS)
     at_high = jnp.floor(at * 0.5)
@@ -313,30 +355,25 @@
     group_of_ref[...] = digits[0:elems].astype(I32)
     at_ref[...] = (2.0 * digits[elems : 2 * elems] + digits[2 * elems :]).astype(I32)
 
+    index = (nb_ref[...] - jnp.where(nb_ref[...] >= 0, (me - 1) * elems, 0)).astype(F32)
+    index = jnp.concatenate([index, jnp.zeros((2, elems), F32)], axis=0)
+    index = jnp.concatenate([index] * (LANES // elems), axis=1).T[0:elems]
+    columns = lax.broadcasted_iota(I32, (elems, 3 * elems), 1).astype(F32)
+    column = [jnp.broadcast_to(index[:, f : f + 1], (elems, 3 * elems)) for f in range(6)]
+    picker = jnp.concatenate([jnp.where(columns == column[f], 1.0, 0.0) for f in range(6)], axis=0).astype(BF16)
+    picker_ref[...] = picker
+    present = [jnp.where(index[:, f : f + 1] >= 0, 0.5, 0.0) for f in range(6)]
+    present_ref[...] = jnp.concatenate([jnp.broadcast_to(p, (elems, 64)) for p in present], axis=1)
+
     elem_rows = row_ref[0:elems, :]
     together = 4
-    turns = half // together
-
-    @pl.loop(0, 2 * turns)
-    def _(it):
-        w, turn = it // turns, lax.rem(it, turns)
-
-        @pl.when(it == turns)
-        def _():
-            table_copy.wait_recv()
-            halve(1, mirror_ref)
-
-        sources = []
-        for u in range(together):
-            s = together * turn + u
-            s = s + w * (half - 1 - 2 * s)
-            sources.append(s)
-
-            @pl.when(s > 0)
-            def _():
+    middle = half - 2
+
+    def serve(sources):
+        for w, s in sources:
+            if not isinstance(s, int) or s > 0:
                 incoming(w, s).wait_recv()
-
-        for s in sources:
+        for w, s in sources:
             base = (w * half + (mine ^ s)) * tiles_each
 
             def store(t, value):
@@ -345,10 +382,27 @@
             interpolate(
                 elems, lambda t: arrived[base + t], store, tiles_each, chunk, stacked.at[w], lag_ref, elem_rows
             )
-        for s in sources:
-            @pl.when(s > 0)
-            def _():
+        for w, s in sources:
+            if not isinstance(s, int) or s > 0:
                 reply(w, s).start()
+
+    serve([(0, 0), (0, 1)])
+
+    @pl.loop(0, 2 * middle // together)
+    def _(it):
+        @pl.when(it == middle // together)
+        def _():
+            table_copy.wait_recv()
+            halve(1, mirror_ref)
+
+        sources = []
+        for u in range(together):
+            i = it * together + u
+            w = i // middle
+            sources.append((w, 2 + i + w * (2 * half - 5 - 2 * i)))
+        serve(sources)
+
+    serve([(1, 1), (1, 0)])
 
     for w in range(2):
         own = (w * half + mine) * tiles_each
@@ -408,7 +462,7 @@
     def _():
         above[...] = jnp.zeros_like(above)
 
-    step = 4
+    step = face_elems
     per_chunk = face_elems // step
 
     @pl.loop(0, elems // step)
@@ -436,14 +490,6 @@
             inner_ref[c, pl.ds(it * step + u, 1), :] = value
 
         pick(it * step, step, 384, inside, store)
-
-    index = (nb_ref[...] - jnp.where(nb_ref[...] >= 0, (me - 1) * elems, 0)).astype(F32)
-    index = jnp.concatenate([index, jnp.zeros((2, elems), F32)], axis=0)
-    index = jnp.concatenate([index] * (LANES // elems), axis=1).T[0:elems]
-    columns = lax.broadcasted_iota(I32, (elems, 3 * elems), 1).astype(F32)
-    column = [jnp.broadcast_to(index[:, f : f + 1], (elems, 3 * elems)) for f in range(6)]
-    picker = jnp.concatenate([jnp.where(columns == column[f], 1.0, 0.0) for f in range(6)], axis=0).astype(BF16)
-    present = [jnp.where(index[:, f : f + 1] >= 0, 0.5, 0.0) for f in range(6)]
 
     for w in range(2):
         @pl.loop(1, half)
@@ -468,15 +514,6 @@
             axis=1,
         )
 
-    own = [whole(faces, c) for c in range(3)]
-    present = jnp.concatenate([jnp.broadcast_to(p, (elems, 64)) for p in present], axis=1)
-    middle = across_of(picker[:, elems : 2 * elems], own)
-    base = [0.5 * moved(middle, c) - present * own[c] for c in range(3)]
-    kept = jnp.concatenate([jnp.concatenate([own[c], inner_ref[c]], axis=1) for c in range(3)], axis=0)
-    hi, lo = halves_of(kept)
-    spread = dot(jnp.concatenate([hi, lo], axis=0), back_ref[...])
-    vals[...] = spread[: 3 * elems] + spread[3 * elems :]
-
     for q in range(FACE_CHUNKS):
         @pl.when(me < peers - 1)
         def _():
@@ -488,14 +525,17 @@
             face_copy(q, 1).wait_send()
             face_copy(q, 0).wait_recv()
 
-    picks = jnp.concatenate([picker[:, :elems], picker[:, 2 * elems :]], axis=1)
-    outside = [jnp.concatenate([whole(below, c), whole(above, c)], axis=0) for c in range(3)]
-    outside = across_of(picks, outside)
-    hi, lo = halves_of(jnp.concatenate([base[c] + 0.5 * moved(outside, c) for c in range(3)], axis=0))
-    spread = dot(jnp.concatenate([hi, lo], axis=0), sel_t_ref[...])
+    own = [whole(faces, c) for c in range(3)]
+    extended = [jnp.concatenate([whole(below, c), own[c], whole(above, c)], axis=0) for c in range(3)]
+    across = across_of(picker_ref[...], extended)
+    present = present_ref[...]
+    changes = [0.5 * moved(across, c) - present * own[c] for c in range(3)]
+    hi, lo = halves_of(
+        jnp.concatenate([jnp.concatenate([own[c], inner_ref[c], changes[c]], axis=1) for c in range(3)], axis=0)
+    )
+    spread = dot(jnp.concatenate([hi, lo], axis=0), back_ref[...])
     for c in range(3):
-        rows = slice(c * elems, (c + 1) * elems)
-        out_ref[c] = vals[rows] + (spread[rows] + spread[(c + 3) * elems : (c + 4) * elems])
+        out_ref[c] = spread[c * elems : (c + 1) * elems] + spread[(c + 3) * elems : (c + 4) * elems]
 
 
 def advect(velocity, coords, owner, elem, neighbours, outer, inner):
@@ -510,17 +550,23 @@
     sorted_tiles = used + tiles_each
     groups = round_up(used * LANES, PICK_ROWS * 8) // PICK_ROWS
     code_lanes = round_up(groups * PICK_ROWS // LANES, LANES)
-    tri = np.concatenate([np.triu(np.ones((LANES, LANES))), np.ones((LANES, LANES))], axis=1)
-    low = np.tril(np.ones((points // LANES, points // LANES)), -1)
-    order, back, sel_t = node_split()
+    tri = np.concatenate([np.triu(np.ones((LANES, LANES)), 1), np.ones((LANES, LANES))], axis=1)
+    low = np.tril(np.ones((points // LANES, points // LANES)))
+    order, back = node_split()
     face_block = (FACE_CHUNKS, 3, elems // FACE_CHUNKS, 384)
     vmem = pl.BlockSpec(memory_space=pltpu.VMEM)
+    operands = (
+        owner, jnp.asarray(tri, BF16), jnp.asarray(low, BF16), velocity, coords, elem, neighbours,
+        jnp.asarray(lagrange_constants()), jnp.asarray(order, BF16), jnp.asarray(back, BF16),
+    )
     return pl.pallas_call(
         functools.partial(advect_kernel, outer, inner, tiles_each, sorted_tiles, min(capacity, 256)),
-        in_specs=[vmem] * 11,
+        in_specs=[pl.BlockSpec(memory_space=pltpu.HBM)] * len(operands),
         out_specs=vmem,
         out_shape=jax.ShapeDtypeStruct((3, elems, 512), F32),
-        scratch_shapes=[
+        scratch_shapes=[pltpu.VMEM(x.shape, x.dtype) for x in operands]
+        + [
+            pltpu.SemaphoreType.DMA((len(operands),)),
             pltpu.VMEM((points // LANES, LANES), F32),
             pltpu.VMEM((1, LANES + code_lanes), I32),
             pltpu.SMEM((1, LANES + code_lanes), I32),
@@ -537,13 +583,14 @@
             pltpu.VMEM((peers * tiles_each, 4, LANES), F32),
             pltpu.VMEM((PICK_ROWS // LANES, 4 * groups, LANES), F32),
             pltpu.VMEM((6 * groups, PICK_ROWS), BF16),
-            pltpu.VMEM((3 * elems, 512), F32),
             pltpu.VMEM(face_block, F32),
             pltpu.VMEM(face_block, F32),
             pltpu.VMEM(face_block, F32),
             pltpu.VMEM((elems, order.shape[1]), I32),
             pltpu.VMEM((elems, order.shape[1]), I32),
             pltpu.VMEM((3, elems, order.shape[1] - 384), F32),
+            pltpu.VMEM((6 * elems, 3 * elems), BF16),
+            pltpu.VMEM((elems, 384), F32),
             pltpu.SemaphoreType.DMA,
             pltpu.SemaphoreType.DMA,
             pltpu.SemaphoreType.DMA,
@@ -552,11 +599,7 @@
         + [pltpu.SemaphoreType.DMA((FACE_CHUNKS, 2))] * 2,
         compiler_params=pltpu.CompilerParams(collective_id=0, has_side_effects=True),
         name="advect",
-    )(
-        velocity, coords, owner, elem, neighbours, jnp.asarray(tri, BF16), jnp.asarray(low, BF16),
-        jnp.asarray(lagrange_constants()),
-        jnp.asarray(order, BF16), jnp.asarray(back, BF16), jnp.asarray(sel_t, BF16),
-    )
+    )(*operands)
 
 
 def local(velocity, depart, owner_rank, owner_element_index, neighbours):

time: 48.7 us -> 44 us (0.903)
  Pallas kernels: 46.9 us -> 42.2 us
    pallas_call x1, Pallas kernels: 46.9 us -> 42.2 us  [advect(): pl.pallas_call(functools.partial(advect_kernel, outer, inner, tiles_each,...]
where the time goes in v3:
time: 44 us; the launch traced here: 43.8 us
  Pallas kernels  42.2 us (96%)
  local copies, waits for them, and re-layouts  1.62 us (4%)
    pallas_call x1, Pallas kernels, advect(): pl.pallas_call(functools.partial(advect_kernel, outer, inner, tiles_each,...  42.2 us
    unnamed x1, local copies, waits for them, and re-layouts  1.62 us

profile of v3, /device:TPU:0, one launch (start us, length us, event | category | flops | bytes accessed | tf_op | source)
XLA Modules:
  0.0 43.8 jit_solution(5147618207035485444)
XLA Ops:
  0.0 42.2 %advect.1 = f32[3,32,512]{2,1,0:T(8,128)} custom-call(s32[128,128]{1,0:T(8,128)} %bitcast.2, bf16[128,256]{1,0:T(8,128)(2,1)} %constant.10.clone.tri_hbm, bf16[128,128]{1,0:T(8,128)(2,1)} %constant.11.clone.low_hbm, f32[3,32,512]{2,1,0:T(8,128)} %vel_hbm.1, f32[3,16384]{1,0:T(4,128)} %coords_hbm.1, s32[128,128]{1,0:T(8,128)} %bitcast.3, s32[6,32]{1,0:T(8,128)} %nb_hbm.1, ...), custom_call_target="tpu_custom_call" | custom-call | tf_op jit(solution)/shard_map/advect/pallas_call | solution.py:562
  42.2 1.6 %copy.12 = f32[3,32,512]{2,1,0:T(8,128)} copy(f32[3,32,512]{2,1,0:T(8,128)} %advect.1) | data formatting | bytes 393216

commit v4 on v3

--- a/solution.py
+++ b/solution.py
@@ -259,7 +259,7 @@
     outer_edge = (edge == 0) | (edge == 3)
 
     load(4, 2)
-    span = 32
+    span = 64
     steps = points // LANES // span
 
     def ahead(it):
@@ -271,11 +271,11 @@
         def _():
             table_copy.start()
 
-        @pl.when((it == steps - 1) & jnp.logical_not(outer_edge))
-        def _():
-            table_copy.start()
-
     place(span, steps, ahead, pos_ref, coords_ref, elem_ref, row_ref, group_ref, acc)
+
+    @pl.when(jnp.logical_not(outer_edge))
+    def _():
+        table_copy.start()
 
     per_group = size // LANES
     for j in range(per_group):
@@ -366,7 +366,7 @@
     present_ref[...] = jnp.concatenate([jnp.broadcast_to(p, (elems, 64)) for p in present], axis=1)
 
     elem_rows = row_ref[0:elems, :]
-    together = 4
+    together = 7
     middle = half - 2
 
     def serve(sources):

time: 44 us -> 43.3 us (0.984)
  Pallas kernels: 42.2 us -> 41.2 us
    pallas_call x1, Pallas kernels: 42.2 us -> 41.2 us  [advect(): pl.pallas_call(functools.partial(advect_kernel, outer, inner, tiles_each,...]
where the time goes in v4:
time: 43.3 us; the launch traced here: 42.8 us
  Pallas kernels  41.2 us (95%)
  local copies, waits for them, and re-layouts  1.62 us (4%)
    pallas_call x1, Pallas kernels, advect(): pl.pallas_call(functools.partial(advect_kernel, outer, inner, tiles_each,...  41.2 us
    unnamed x1, local copies, waits for them, and re-layouts  1.62 us

profile of v4, /device:TPU:0, one launch (start us, length us, event | category | flops | bytes accessed | tf_op | source)
XLA Modules:
  0.0 42.8 jit_solution(6192976449331882198)
XLA Ops:
  0.0 41.2 %advect.1 = f32[3,32,512]{2,1,0:T(8,128)} custom-call(s32[128,128]{1,0:T(8,128)} %bitcast.2, bf16[128,256]{1,0:T(8,128)(2,1)} %constant.10.clone.tri_hbm, bf16[128,128]{1,0:T(8,128)(2,1)} %constant.11.clone.low_hbm, f32[3,32,512]{2,1,0:T(8,128)} %vel_hbm.1, f32[3,16384]{1,0:T(4,128)} %coords_hbm.1, s32[128,128]{1,0:T(8,128)} %bitcast.3, s32[6,32]{1,0:T(8,128)} %nb_hbm.1, ...), custom_call_target="tpu_custom_call" | custom-call | tf_op jit(solution)/shard_map/advect/pallas_call | solution.py:562
  41.2 1.6 %copy.12 = f32[3,32,512]{2,1,0:T(8,128)} copy(f32[3,32,512]{2,1,0:T(8,128)} %advect.1) | data formatting | bytes 393216
